TPU v7x, 32 devices: a whole 2x2x4 slice. The times are simulated.
32 devices in a mesh: dp: 8 (over z, y), tp: 4 (over x, core).
Axes of the slice: x: 2, y: 2, z: 4, core: 2. Of those that a mesh axis runs over, the one named last changes fastest.
Arguments:
- tokens: bfloat16 [768, 2880], P('dp', 'tp'), may hold values from -100 to 100
- attn_gain: float32 [2880], replicated, may hold values from 0.1 to 1.9
- w_query: bfloat16 [2880, 2048], P(None, 'tp'), may hold values from -0.109375 to 0.109375
- w_keyvalue: bfloat16 [2880, 8, 128], P(None, 'tp'), may hold values from -0.109375 to 0.109375
- attn_sinks: float32 [32], P('tp'), may hold values from 2 to 6
- w_out: bfloat16 [2048, 2880], P('tp'), may hold values from -0.125 to 0.125
- window_cache: bfloat16 [768, 8, 128, 128], P('dp', 'tp'), may hold values from -1000 to 1000
- positions: int32 [768], P('dp'), may hold values from 0 to 511
- moe_gain: float32 [2880], replicated, may hold values from 0.1 to 1.9
- router: bfloat16 [2880, 8], P('tp'), may hold values from -0.109375 to 0.109375
- gate_up: bfloat16 [8, 2880, 2, 2880], P('dp', None, None, 'tp'), may hold values from -0.109375 to 0.109375
- w_down: bfloat16 [8, 2880, 2880], P('dp', None, 'tp'), may hold values from -0.109375 to 0.109375
- expert_ids: int32 [768, 4], P('dp'), may hold values from 0 to 7, all different within a row; in each aligned block of 96 rows (0 to 95, 96 to 191, ...) at most 96 rows name the same one
Outputs:
- layer_out: float32 [768, 2880], P('dp', 'tp')
Inputs may be any that keep to these rules, and one draw needn't show every extreme that they name: `expert_ids`: each row names 4 different experts. Within the rows of one index of dp no expert is named by more than 96 rows, a bound that some of these blocks reach.
All inputs are finite; a program needn't handle non-finite values.
Results may differ from a plain program's by a relative error of at most 0.0066.
Values may be sent and summed in bfloat16 or wider, within the bound.
A program may use at most 128 MiB of HBM per device.

v0:
```python
import jax
import jax.numpy as jnp
from jax import lax
from jax.sharding import PartitionSpec as P

norm_eps = 1e-05
rope_base = 150000.0
glu_alpha = 1.702


def rope_tables(positions, head_size):
    half_size = head_size // 2
    exponent = jnp.arange(half_size, dtype=jnp.float32) * (2.0 / head_size)
    inverse = jnp.power(jnp.float32(rope_base), -exponent)
    angles = positions.astype(jnp.float32)[:, None] * inverse[None, :]
    return (jnp.cos(angles), jnp.sin(angles))


def rotate(values, cosine, sine_table):
    half_size = values.shape[-1] // 2
    first_half = values[..., :half_size]
    second_half = values[..., half_size:]
    return jnp.concatenate(
        [
            first_half * cosine - second_half * sine_table,
            second_half * cosine + first_half * sine_table,
        ],
        axis=-1,
    )


def on_device(
    tokens,
    attn_gain,
    w_query,
    w_keyvalue,
    attn_sinks,
    w_out,
    window_cache,
    positions,
    moe_gain,
    router,
    gate_up,
    w_down,
    expert_ids,
):
    tp_count = lax.axis_size("tp")
    dp_count = lax.axis_size("dp")
    seq_count, col_count = tokens.shape
    full_width = col_count * tp_count
    col_start = lax.axis_index("tp") * col_count
    head_size = w_keyvalue.shape[2] // 2
    kv_local = w_keyvalue.shape[1]
    q_local = w_query.shape[1] // head_size
    group_size = q_local // kv_local
    window = window_cache.shape[2]
    attn_slice = lax.dynamic_slice_in_dim(attn_gain, col_start, col_count)
    moe_slice = lax.dynamic_slice_in_dim(moe_gain, col_start, col_count)
    tok_wide = tokens.astype(jnp.float32)
    attn_sq = lax.psum(jnp.sum(tok_wide * tok_wide, axis=1), "tp")
    normed = (
        tok_wide * lax.rsqrt(attn_sq / full_width + norm_eps)[:, None] * attn_slice[None, :]
    ).astype(jnp.bfloat16)
    kv_flat = w_keyvalue.reshape(full_width, kv_local * 2 * head_size)
    piece_rows = lax.all_gather(normed, "tp", axis=1, tiled=True)
    queries = jnp.dot(piece_rows, w_query, preferred_element_type=jnp.float32)
    fresh_rows = jnp.dot(piece_rows, kv_flat, preferred_element_type=jnp.float32)
    cosine, sine_table = rope_tables(positions, head_size)
    rot_queries = rotate(
        queries.reshape(seq_count, q_local, head_size), cosine[:, None, :], sine_table[:, None, :]
    ).astype(jnp.bfloat16)
    fresh_rows = fresh_rows.reshape(seq_count, kv_local, 2 * head_size)
    new_key = rotate(fresh_rows[..., :head_size], cosine[:, None, :], sine_table[:, None, :])
    new_entry = jnp.concatenate([new_key, fresh_rows[..., head_size:]], axis=-1).astype(
        jnp.bfloat16
    )
    slot_ids = jnp.arange(window, dtype=jnp.int32)
    is_current = slot_ids[None, :] == (positions % window)[:, None]
    cache_now = jnp.where(is_current[:, None, :, None], new_entry[:, :, None, :], window_cache)
    is_valid = (positions[:, None] - slot_ids[None, :]) % window <= positions[:, None]
    grouped = rot_queries.reshape(seq_count, kv_local, group_size, head_size)
    scores = jnp.einsum(
        "skgh,skwh->skgw", grouped, cache_now[..., :head_size], preferred_element_type=jnp.float32
    ) * head_size ** (-0.5)
    scores = jnp.where(is_valid[:, None, None, :], scores, -jnp.inf)
    sink_col = attn_sinks.reshape(kv_local, group_size)[None, :, :, None]
    peak_score = jnp.maximum(jnp.max(scores, axis=-1, keepdims=True), sink_col)
    raised = jnp.exp(scores - peak_score)
    denominator = jnp.sum(raised, axis=-1, keepdims=True) + jnp.exp(sink_col - peak_score)
    prob_bf = (raised / denominator).astype(jnp.bfloat16)
    attended = jnp.einsum(
        "skgw,skwh->skgh", prob_bf, cache_now[..., head_size:], preferred_element_type=jnp.float32
    ).astype(jnp.bfloat16)
    partial_out = jnp.dot(
        attended.reshape(seq_count, q_local * head_size), w_out, preferred_element_type=jnp.float32
    )
    residual = tok_wide + lax.psum_scatter(
        partial_out.astype(jnp.bfloat16), "tp", scatter_dimension=1, tiled=True
    ).astype(jnp.float32)
    experts = router.shape[1]
    top_count = expert_ids.shape[1]
    local_experts = gate_up.shape[0]
    ff_local = gate_up.shape[3]
    capacity = min(seq_count, max(2, 8 * seq_count * top_count // (3 * experts)))
    moe_sq = jnp.sum(residual * residual, axis=1)
    router_wide = router.astype(jnp.float32)
    total_sq = lax.psum(moe_sq, "tp")
    moe_scale = lax.rsqrt(total_sq / full_width + norm_eps)[:, None]
    scaled = residual * moe_scale * moe_slice[None, :]
    logits = lax.psum(jnp.dot(scaled, router_wide, precision=lax.Precision.HIGHEST), "tp")
    hidden_rows = scaled.astype(jnp.bfloat16)
    expert_iota = jnp.arange(experts, dtype=jnp.int32)
    chosen = expert_ids[:, :, None] == expert_iota[None, None, :]
    picked = jnp.sum(jnp.where(chosen, logits[:, None, :], 0.0), axis=-1)
    raised_logits = jnp.exp(picked)
    route_weights = raised_logits / jnp.sum(raised_logits, axis=1, keepdims=True)
    assign = expert_ids.reshape(-1)
    onehot = (assign[:, None] == expert_iota[None, :]).astype(jnp.int32)
    earlier = jnp.cumsum(onehot, axis=0) - onehot
    slot_of = jnp.sum(earlier * onehot, axis=1)
    target = (assign * capacity + slot_of).reshape(seq_count, top_count)
    spot_ids = jnp.arange(experts * capacity, dtype=jnp.int32)
    slot_hits = target[:, :, None] == spot_ids[None, None, :]
    placer = jnp.transpose(jnp.any(slot_hits, axis=1)).astype(jnp.bfloat16)
    combiner = jnp.sum(jnp.where(slot_hits, route_weights[:, :, None], 0.0), axis=1)
    gate_up_flat = gate_up.reshape(local_experts, full_width, 2 * ff_local)
    placed = jnp.dot(placer, hidden_rows, preferred_element_type=jnp.float32).astype(jnp.bfloat16)
    mixed_in = jnp.einsum(
        "gecd,edf->gecf",
        lax.all_gather(
            lax.all_to_all(
                placed.reshape(dp_count, local_experts, capacity, hidden_rows.shape[1]),
                "dp",
                split_axis=0,
                concat_axis=0,
                tiled=True,
            ),
            "tp",
            axis=3,
            tiled=True,
        ),
        gate_up_flat,
        preferred_element_type=jnp.float32,
    )
    gate_part = mixed_in[..., :ff_local]
    up_part = mixed_in[..., ff_local:]
    act_rows = (gate_part * jax.nn.sigmoid(glu_alpha * gate_part) * (up_part + 1.0)).astype(
        jnp.bfloat16
    )
    answered = jnp.einsum(
        "gecf,efd->gecd",
        lax.all_gather(act_rows, "tp", axis=3, tiled=True),
        w_down,
        preferred_element_type=jnp.float32,
    ).astype(jnp.bfloat16)
    returned = lax.all_to_all(answered, "dp", split_axis=0, concat_axis=0, tiled=True)
    flat_back = returned.reshape(experts * capacity, col_count).astype(jnp.float32)
    moe_out = jnp.dot(combiner, flat_back, precision=lax.Precision.HIGHEST)
    return residual + moe_out


def solution(mesh):
    in_specs = (
        P("dp", "tp"),
        P(),
        P(None, "tp"),
        P(None, "tp", None),
        P("tp"),
        P("tp", None),
        P("dp", "tp", None, None),
        P("dp"),
        P(),
        P("tp", None),
        P("dp", None, None, "tp"),
        P("dp", None, "tp"),
        P("dp", None),
    )
    out_specs = P("dp", "tp")
    return jax.shard_map(
        on_device, mesh=mesh, in_specs=in_specs, out_specs=out_specs, check_vma=False
    )
```

profile of v0, /device:TPU:0, one launch (start us, length us, event | category | flops | bytes accessed | tf_op | source)
XLA Modules:
  0.0 306.0 jit_solution(1373459359515891442)
XLA Ops:
  6.6 1.2 fusion.37
  7.8 8.4 %psum.21 = f32[96]{0:T(128)S(1)} all-reduce(f32[96]{0:T(128)S(1)} %fusion.37), channel_id=1, replica_groups=mesh['dp'=8,'tp'=4] {'tp'}, use_global_device_ids=true, to_apply=%region_1.0 | all-reduce | flops 96 | bytes 768 | tf_op jit(solution)/shard_map/psum | solution.py:60
  16.1 0.8 dynamic_slice.6
  16.9 1.0 fusion.48
  17.9 6.7 %all-gather = bf16[4,720,96]{1,2,0:T(8,128)(2,1)S(1)} all-gather(bf16[1,720,96]{1,2,0:T(8,128)(2,1)S(1)} %fusion.48), channel_id=1, replica_groups=mesh['dp'=8,'tp'=4] {'tp'}, dimensions={0}, use_global_device_ids=true | all-gather | bytes 691200 | tf_op jit(solution)/shard_map/all_gather | solution.py:65
  24.6 0.5 copy.86
  25.1 1.3 reshape.248
  26.4 1.3 reshape.247
  27.6 0.5 fusion.63
  28.2 0.7 fusion.54
  28.9 4.9 %copy.111 = bf16[2880,2,128]{0,2,1:T(8,128)(2,1)} copy(bf16[2880,2,128]{2,1,0:T(2,128)(2,1)} %param.16) | data formatting | bytes 2949120 | tf_op jit(solution)/shard_map/dot_general | solution.py:67
  33.7 0.1 multiply_cosine_fusion
  33.9 0.7 copy.92
  34.6 0.7 copy.93
  35.3 2.0 fusion.19
  37.3 0.1 slice.84
  37.4 0.9 subtract_convert_fusion.1
  38.3 0.1 pad_maximum_fusion
  38.4 0.7 copy.94
  39.1 1.3 iota_compare_fusion.1
  40.4 8.7 %copy.95 = bf16[96,2,128,128]{2,3,1,0:T(8,128)(2,1)} copy(bf16[96,2,128,128]{3,2,1,0:T(8,128)(2,1)} %param.19) | data formatting | bytes 12582912 | tf_op args[6]
  49.1 3.1 %fusion.65 = f32[96,512]{0,1:T(8,128)S(1)} fusion(bf16[2880,96]{0,1:T(8,128)(2,1)S(1)} %copy-done.3, bf16[2880,512]{1,0:T(8,128)(2,1)} %param.15), kind=kOutput, calls=%fused_computation.91 | convolution fusion | flops 283115520 | bytes 3698688 | tf_op jit(solution)/shard_map/dot_general | solution.py:66
  52.3 0.2 copy.88
  52.4 0.2 copy.89
  52.6 0.1 max.18
  52.7 7.2 %broadcast_select_fusion = bf16[96,2,128,128]{2,3,1,0:T(8,128)(2,1)S(1)} fusion(bf16[96,2,128,128]{2,3,1,0:T(8,128)(2,1)} %copy.95, pred[96,128]{1,0:T(8,128)(4,1)} %iota_compare_fusion.1, bf16[96,2,128]{2,1,0:T(2,128)(2,1)} %copy.94), kind=kLoop, calls=%fused_computation | loop fusion | flops 3145728 | bytes 12644352 | tf_op jit(solution)/shard_map/jit(_where)/select_n | solution.py:79
  59.9 1.2 fusion.64
  61.2 0.6 fusion.36
  61.8 1.8 fusion.33
  63.6 0.2 copy.96
  63.8 1.9 convolution_convert_fusion
  65.7 2.2 copy.112
  68.0 0.1 copy.97
  68.1 0.1 eq.76
  68.2 0.1 eq.72
  68.3 0.8 dynamic_slice.7
  69.1 0.8 reduce-window.6
  69.9 0.2 slice_reduce_fusion
  70.2 0.1 fusion.59
  70.3 0.1 reduce_sum.68
  70.5 0.2 fusion.32
  70.7 21.4 %reduce-scatter.4.cloned.1.call-done = bf16[720,96]{1,0:T(8,128)(2,1)} async-done(((bf16[2880,96]{1,0:T(8,128)(2,1)}), bf16[720,96]{1,0:T(8,128)(2,1)}) %reduce-scatter.4.cloned.1.call-update) | async-done | bytes 138256
  92.1 1.0 copy.113
  93.2 0.1 multiply_reduce_fusion
  93.3 5.8 %psum.22 = f32[96]{0:T(128)S(1)} all-reduce(f32[96]{0:T(128)S(1)} %multiply_reduce_fusion), channel_id=1, replica_groups=mesh['dp'=8,'tp'=4] {'tp'}, use_global_device_ids=true, to_apply=%region_9.10 | all-reduce | flops 96 | bytes 768 | tf_op jit(solution)/shard_map/psum | solution.py:107
  99.1 0.6 convolution_convert_fusion.1
  99.7 0.6 copy.100
  100.3 34.2 %all_to_all.10 = bf16[8,1,96,720]{3,2,1,0:T(8,128)(2,1)S(1)} all-to-all(bf16[8,1,96,720]{3,2,1,0:T(8,128)(2,1)S(1)} %bitcast.88), channel_id=1, replica_groups=mesh['dp'=8,'tp'=4] {'dp'}, dimensions={0} | all-to-all | bytes 2211840 | tf_op jit(solution)/shard_map/all_to_all | solution.py:131
  134.5 1.9 copy.102
  136.5 0.2 all-gather.6.cloned.1.call-start
  136.7 41.8 %all-gather.4.cloned.1.call-done = bf16[8,1,96,2880]{2,0,1,3:T(8,128)(2,1)} async-done(((bf16[8,1,96,720]{2,0,1,3:T(8,128)(2,1)}), bf16[8,1,96,2880]{2,0,1,3:T(8,128)(2,1)}) %all-gather.4.cloned.1.call-update) | async-done | bytes 4423696 | tf_op jit(solution)/shard_map/all_gather | solution.py:130
  178.5 8.3 %copy.103 = bf16[8,1,96,2880]{3,2,0,1:T(8,128)(2,1)} copy(bf16[8,1,96,2880]{2,0,1,3:T(8,128)(2,1)} %all-gather.4.cloned.1.call-done) | data formatting | bytes 8847360 | tf_op jit(solution)/shard_map/all_gather | solution.py:130
  186.8 11.4 %fusion.5 = f32[8,1,96,1440]{3,2,0,1:T(8,128)S(1)} fusion(bf16[2880,1440,1]{0,1,2:T(8,128)(2,1)} %bitcast.104, bf16[8,1,96,2880]{3,2,0,1:T(8,128)(2,1)} %copy.103), kind=kOutput, calls=%fused_computation.6 | convolution fusion | flops 6370099200 | bytes 17141760 | tf_op jit(solution)/shard_map/gecd,edf->gecf/dot_general | solution.py:128
  198.2 0.8 fusion.13
  199.1 1.9 copy.104
  201.0 44.3 %all-gather.6.cloned.1.call-done = bf16[8,1,96,2880]{2,0,1,3:T(8,128)(2,1)} async-done(((bf16[8,1,96,720]{2,0,1,3:T(8,128)(2,1)}), bf16[8,1,96,2880]{2,0,1,3:T(8,128)(2,1)}) %all-gather.6.cloned.1.call-update) | async-done | bytes 4423696 | tf_op jit(solution)/shard_map/all_gather | solution.py:152
  245.3 8.3 %copy.105 = bf16[8,1,96,2880]{3,2,0,1:T(8,128)(2,1)} copy(bf16[8,1,96,2880]{2,0,1,3:T(8,128)(2,1)} %all-gather.6.cloned.1.call-done) | data formatting | bytes 8847360 | tf_op jit(solution)/shard_map/all_gather | solution.py:152
  253.6 8.6 %fusion.21 = bf16[8,1,96,720]{3,2,1,0:T(8,128)(2,1)} fusion(bf16[1,2880,720]{1,2,0:T(8,128)(2,1)} %param.24, bf16[8,1,96,2880]{3,2,0,1:T(8,128)(2,1)} %copy.105), kind=kOutput, calls=%fused_computation.19 | convolution fusion | flops 3185602560 | bytes 9676800 | tf_op jit(solution)/shard_map/gecf,efd->gecd/dot_general | solution.py:150
  262.2 5.5 %all-to-all-start.1 = ((bf16[8,1,96,720]{3,2,1,0:T(8,128)(2,1)}), bf16[8,1,96,720]{3,2,1,0:T(8,128)(2,1)}, u32[]{:S(2)}, u32[]{:S(2)}) async-start(bf16[8,1,96,720]{3,2,1,0:T(8,128)(2,1)} %fusion.21), calls=%async_computation.1 | async-start | bytes 2359296 | tf_op jit(solution)/shard_map/all_to_all | solution.py:156
  267.7 0.3 fusion.41
  268.0 6.2 %psum.23 = f32[96,8]{0,1:T(8,128)S(1)} all-reduce(f32[96,8]{0,1:T(8,128)S(1)} %fusion.41), channel_id=1, replica_groups=mesh['dp'=8,'tp'=4] {'tp'}, use_global_device_ids=true, to_apply=%region_10.11 | all-reduce | flops 768 | bytes 6144 | tf_op jit(solution)/shard_map/psum | solution.py:110
  274.3 0.2 select_reduce_fusion
  274.5 22.3 %all-to-all-done.1 = bf16[8,1,96,720]{3,2,1,0:T(8,128)(2,1)} async-done(((bf16[8,1,96,720]{3,2,1,0:T(8,128)(2,1)}), bf16[8,1,96,720]{3,2,1,0:T(8,128)(2,1)}, u32[]{:S(2)}, u32[]{:S(2)}) %all-to-all-start.1) | async-done | bytes 1105952 | tf_op jit(solution)/shard_map/all_to_all | solution.py:156
  296.8 2.7 convolution_add_fusion
  (40 shorter events, 0.4 us)
Async XLA Ops:
  6.5 57.3 %copy-start = (bf16[512,2880]{0,1:T(8,128)(2,1)S(1)}, bf16[512,2880]{0,1:T(8,128)(2,1)}, u32[]{:S(2)}) copy-start(bf16[512,2880]{0,1:T(8,128)(2,1)} %param.18) | copy-start | bytes 8847364
  6.5 21.1 %copy-start.7 = (s32[96]{0:T(128)S(1)}, s32[96]{0:T(128)}, u32[]{:S(2)}) copy-start(s32[96]{0:T(128)} %param.20) | copy-start | bytes 1156
  6.5 85.6 %reduce-scatter.4.cloned.1.call-start = ((), (), s32[]{:S(2)}) async-start(), calls=%async_computation.5 | async-start | bytes 921600
  27.6 7.7 %copy-start.4 = (bf16[2880,96,1]{0,1,2:T(8,128)(2,1)S(1)}, bf16[2880,96,1]{0,1,2:T(8,128)(2,1)}, u32[]{:S(2)}) copy-start(bf16[2880,96,1]{0,1,2:T(8,128)(2,1)} %reshape.248) | copy-start | bytes 1658884
  40.4 8.7 %copy-start.3 = (bf16[2880,96]{0,1:T(8,128)(2,1)S(1)}, bf16[2880,96]{0,1:T(8,128)(2,1)}, u32[]{:S(2)}) copy-start(bf16[2880,96]{0,1:T(8,128)(2,1)} %reshape.247) | copy-start | bytes 1658884
  49.1 3.5 %copy-start.9 = (f32[8]{0:T(128)S(1)}, f32[8]{0:T(128)}, u32[]{:S(2)}) copy-start(f32[8]{0:T(128)} %param.17) | copy-start | bytes 100
  52.7 7.2 %copy-start.6 = (pred[96,128]{1,0:T(8,128)(4,1)S(1)}, pred[96,128]{1,0:T(8,128)(4,1)}, u32[]{:S(2)}) copy-start(pred[96,128]{1,0:T(8,128)(4,1)} %fusion.54) | copy-start | bytes 36868
  63.6 4.4 %copy-start.5 = (s32[96,4]{0,1:T(4,128)S(1)}, s32[96,4]{0,1:T(4,128)}, u32[]{:S(2)}) copy-start(s32[96,4]{0,1:T(4,128)} %param.25) | copy-start | bytes 4612
  63.8 29.4 %copy-start.2 = (bf16[96,720]{1,0:T(8,128)(2,1)S(1)}, bf16[96,720]{1,0:T(8,128)(2,1)}, u32[]{:S(2)}) copy-start(bf16[96,720]{1,0:T(8,128)(2,1)} %param.13) | copy-start | bytes 414724
  67.9 110.5 %all-gather.4.cloned.1.call-start = ((), (), s32[]{:S(2)}) async-start(), calls=%async_computation.3 | async-start | bytes 7372800 | tf_op jit(solution)/shard_map/all_gather | solution.py:130
  136.5 108.8 %all-gather.6.cloned.1.call-start = ((), (), s32[]{:S(2)}) async-start(), calls=%async_computation.4 | async-start | bytes 7372800 | tf_op jit(solution)/shard_map/all_gather | solution.py:152
  253.6 14.1 %copy-start.8 = (bf16[720,8]{0,1:T(8,128)(2,1)S(1)}, bf16[720,8]{0,1:T(8,128)(2,1)}, u32[]{:S(2)}) copy-start(bf16[720,8]{0,1:T(8,128)(2,1)} %param.22) | copy-start | bytes 34564
  253.6 45.9 %copy-start.1 = (bf16[512,2880]{0,1:T(8,128)(2,1)S(1)}, bf16[512,2880]{0,1:T(8,128)(2,1)}, u32[]{:S(2)}) copy-start(bf16[512,2880]{0,1:T(8,128)(2,1)} %param.18) | copy-start | bytes 8847364
  262.2 34.6 %all-to-all-start.1 = ((bf16[8,1,96,720]{3,2,1,0:T(8,128)(2,1)}), bf16[8,1,96,720]{3,2,1,0:T(8,128)(2,1)}, u32[]{:S(2)}, u32[]{:S(2)}) async-start(bf16[8,1,96,720]{3,2,1,0:T(8,128)(2,1)} %fusion.21), calls=%async_computation.1 | async-start | bytes 2359296 | tf_op jit(solution)/shard_map/all_to_all | solution.py:156
Sparse Core Ops, SparseCore 0:
  68.0 24.0 reduce-scatter.3
  136.6 41.8 all-gather.3
  201.1 44.1 all-gather.5
where the time goes:
time: 307 us; the launch traced here: 306 us
  waiting for transfers between devices  130 us (42%)
  blocking collectives  61.2 us (20%)
  local copies, waits for them, and re-layouts  46.1 us (15%)
  matrix products  33.5 us (11%)
  other arithmetic  16.2 us (5%)
  between operations  13.4 us (4%)
  starting transfers between devices  5.78 us (2%)
    all_gather x1, waiting for transfers between devices, on_device(): lax.all_gather(act_rows, 'tp', axis=3, tiled=True)  44.3 us
    all_gather x1, waiting for transfers between devices, on_device(): lax.all_gather(lax.all_to_all(placed.reshape(dp_count, local_experts, cap...  41.8 us
    all_to_all x1, blocking collectives, on_device(): lax.all_to_all(placed.reshape(dp_count, local_experts, capacity, hidden_r...  34.2 us
    all_to_all x1, waiting for transfers between devices, on_device(): lax.all_to_all(answered, 'dp', split_axis=0, concat_axis=0, tiled=True)  22.3 us
    unnamed x4, waiting for transfers between devices  21.5 us
    unnamed x28, local copies, waits for them, and re-layouts  14.7 us
    dot_general x1, matrix products, on_device(): jnp.einsum('gecd,edf->gecf', lax.all_gather(lax.all_to_all(placed.reshape...  11.4 us
    dot_general x1, matrix products, on_device(): jnp.einsum('gecf,efd->gecd', lax.all_gather(act_rows, 'tp', axis=3, tiled...  8.57 us
  transfers between devices with their start and end apart: 4, of which 4 were waited for; matrix products, arithmetic and copies ran while one was open for 1% of the time, Pallas kernels for 0%

commit v1 on v0

--- a/solution.py
+++ b/solution.py
@@ -6,6 +6,18 @@
 norm_eps = 1e-05
 rope_base = 150000.0
 glu_alpha = 1.702
+
+
+def summed_around(shard, axis, dim, product):
+    size, index, rows = (lax.axis_size(axis), lax.axis_index(axis), shard.shape[dim])
+    upward = [(i, (i + 1) % size) for i in range(size)]
+    held, total = (shard, None)
+    for hop in range(size):
+        coming = lax.ppermute(held, axis, upward) if hop < size - 1 else None
+        absorb = product(held, (index - hop) % size * rows)
+        total = absorb if total is None else total + absorb
+        held = coming
+    return total
 
 
 def rope_tables(positions, head_size):
@@ -147,11 +159,16 @@
     act_rows = (gate_part * jax.nn.sigmoid(glu_alpha * gate_part) * (up_part + 1.0)).astype(
         jnp.bfloat16
     )
-    answered = jnp.einsum(
-        "gecf,efd->gecd",
-        lax.all_gather(act_rows, "tp", axis=3, tiled=True),
-        w_down,
-        preferred_element_type=jnp.float32,
+    answered = summed_around(
+        act_rows,
+        "tp",
+        3,
+        lambda part, at: jnp.einsum(
+            "gecf,efd->gecd",
+            part,
+            lax.dynamic_slice_in_dim(w_down, at, part.shape[3], axis=1),
+            preferred_element_type=jnp.float32,
+        ),
     ).astype(jnp.bfloat16)
     returned = lax.all_to_all(answered, "dp", split_axis=0, concat_axis=0, tiled=True)
     flat_back = returned.reshape(experts * capacity, col_count).astype(jnp.float32)

time: 307 us -> 294 us (0.958)
  local copies, waits for them, and re-layouts: 46.1 us -> 35.8 us
  waiting for transfers between devices: 130 us -> 123 us
  matrix products: 33.5 us -> 37 us
    all_gather x1 -> x0, waiting for transfers between devices: 44.3 us -> none  [on_device(): lax.all_gather(act_rows, 'tp', axis=3, tiled=True)]
    ppermute x0 -> x3, waiting for transfers between devices: none -> 39.1 us  [summed_around(): coming = lax.ppermute(held, axis, upward) if hop < size - 1 else None]
    all_gather x1 -> x0, local copies, waits for them, and re-layouts: 8.35 us -> none  [on_device(): lax.all_gather(act_rows, 'tp', axis=3, tiled=True)]
    dot_general x1 -> x4, matrix products: 8.57 us -> 12 us  [on_device(): jnp.einsum('gecf,efd->gecd', part, lax.dynamic_slice_in_dim(w_down, at, p...]
    unnamed x4 -> x3, waiting for transfers between devices: 21.5 us -> 21.4 us
  transfers between devices with their start and end apart: 4 -> 6, of which waited for: 4 -> 6; matrix products, arithmetic and copies ran while one was open for 1% -> 4% of each run, Pallas kernels for 0% -> 0%
where the time goes in v1:
time: 294 us; the launch traced here: 293 us
  waiting for transfers between devices  123 us (42%)
  blocking collectives  61.1 us (21%)
  matrix products  37 us (13%)
  local copies, waits for them, and re-layouts  35.8 us (12%)
  other arithmetic  16.2 us (6%)
  between operations  13.7 us (5%)
  starting transfers between devices  6 us (2%)
    all_gather x1, waiting for transfers between devices, on_device(): lax.all_gather(lax.all_to_all(placed.reshape(dp_count, local_experts, cap...  42 us
    ppermute x3, waiting for transfers between devices, summed_around(): coming = lax.ppermute(held, axis, upward) if hop < size - 1 else None  39.1 us
    all_to_all x1, blocking collectives, on_device(): lax.all_to_all(placed.reshape(dp_count, local_experts, capacity, hidden_r...  34.2 us
    unnamed x3, waiting for transfers between devices  21.4 us
    all_to_all x1, waiting for transfers between devices, on_device(): lax.all_to_all(answered, 'dp', split_axis=0, concat_axis=0, tiled=True)  20.6 us
    unnamed x28, local copies, waits for them, and re-layouts  14.7 us
    dot_general x4, matrix products, on_device(): jnp.einsum('gecf,efd->gecd', part, lax.dynamic_slice_in_dim(w_down, at, p...  12 us
    dot_general x1, matrix products, on_device(): jnp.einsum('gecd,edf->gecf', lax.all_gather(lax.all_to_all(placed.reshape...  11.4 us
  transfers between devices with their start and end apart: 6, of which 6 were waited for; matrix products, arithmetic and copies ran while one was open for 4% of the time, Pallas kernels for 0%

profile of v1, /device:TPU:0, one launch (start us, length us, event | category | flops | bytes accessed | tf_op | source)
XLA Modules:
  0.0 293.0 jit_solution(1018665786642896984)
XLA Ops:
  6.6 1.2 fusion.40
  7.8 8.4 %psum.21 = f32[96]{0:T(128)S(1)} all-reduce(f32[96]{0:T(128)S(1)} %fusion.40), channel_id=1, replica_groups=mesh['dp'=8,'tp'=4] {'tp'}, use_global_device_ids=true, to_apply=%region_1.0 | all-reduce | flops 96 | bytes 768 | tf_op jit(solution)/shard_map/psum | solution.py:72
  16.1 0.8 dynamic_slice.18
  16.9 1.0 fusion.51
  17.9 6.7 %all-gather = bf16[4,720,96]{1,2,0:T(8,128)(2,1)S(1)} all-gather(bf16[1,720,96]{1,2,0:T(8,128)(2,1)S(1)} %fusion.51), channel_id=1, replica_groups=mesh['dp'=8,'tp'=4] {'tp'}, dimensions={0}, use_global_device_ids=true | all-gather | bytes 691200 | tf_op jit(solution)/shard_map/all_gather | solution.py:77
  24.6 0.5 copy.98
  25.1 1.3 reshape.278
  26.4 1.3 reshape.277
  27.6 0.5 fusion.70
  28.2 0.7 fusion.57
  28.9 4.9 %copy.125 = bf16[2880,2,128]{0,2,1:T(8,128)(2,1)} copy(bf16[2880,2,128]{2,1,0:T(2,128)(2,1)} %param.16) | data formatting | bytes 2949120 | tf_op jit(solution)/shard_map/dot_general | solution.py:79
  33.7 0.1 multiply_cosine_fusion
  33.9 0.7 copy.104
  34.6 0.7 copy.105
  35.3 2.0 fusion.11
  37.4 0.9 subtract_convert_fusion.1
  38.3 0.1 pad_maximum_fusion
  38.4 0.7 copy.106
  39.1 1.3 iota_compare_fusion.1
  40.4 8.7 %copy.107 = bf16[96,2,128,128]{2,3,1,0:T(8,128)(2,1)} copy(bf16[96,2,128,128]{3,2,1,0:T(8,128)(2,1)} %param.19) | data formatting | bytes 12582912 | tf_op args[6]
  49.1 3.1 %fusion.72 = f32[96,512]{0,1:T(8,128)S(1)} fusion(bf16[2880,96]{0,1:T(8,128)(2,1)S(1)} %copy-done.3, bf16[2880,512]{1,0:T(8,128)(2,1)} %param.15), kind=kOutput, calls=%fused_computation.107 | convolution fusion | flops 283115520 | bytes 3698688 | tf_op jit(solution)/shard_map/dot_general | solution.py:78
  52.3 0.2 copy.100
  52.4 0.2 copy.101
  52.7 7.2 %broadcast_select_fusion = bf16[96,2,128,128]{2,3,1,0:T(8,128)(2,1)S(1)} fusion(bf16[96,2,128,128]{2,3,1,0:T(8,128)(2,1)} %copy.107, pred[96,128]{1,0:T(8,128)(4,1)} %iota_compare_fusion.1, bf16[96,2,128]{2,1,0:T(2,128)(2,1)} %copy.106), kind=kLoop, calls=%fused_computation | loop fusion | flops 3145728 | bytes 12644352 | tf_op jit(solution)/shard_map/jit(_where)/select_n | solution.py:91
  59.9 1.2 fusion.71
  61.2 0.6 fusion.39
  61.8 1.8 fusion.28
  63.6 0.2 copy.108
  63.8 1.9 convolution_convert_fusion
  65.7 2.2 copy.126
  68.0 0.1 copy.109
  68.1 0.1 eq.81
  68.2 0.1 eq.77
  68.3 0.8 dynamic_slice.19
  69.1 0.8 reduce-window.6
  69.9 0.2 slice_reduce_fusion
  70.3 0.1 reduce_sum.68
  70.5 0.2 fusion.27
  70.7 21.4 %reduce-scatter.4.cloned.1.call-done = bf16[720,96]{1,0:T(8,128)(2,1)} async-done(((bf16[2880,96]{1,0:T(8,128)(2,1)}), bf16[720,96]{1,0:T(8,128)(2,1)}) %reduce-scatter.4.cloned.1.call-update) | async-done | bytes 138256
  92.2 1.0 copy.127
  93.2 0.1 multiply_reduce_fusion
  93.4 5.8 %psum.22 = f32[96]{0:T(128)S(1)} all-reduce(f32[96]{0:T(128)S(1)} %multiply_reduce_fusion), channel_id=1, replica_groups=mesh['dp'=8,'tp'=4] {'tp'}, use_global_device_ids=true, to_apply=%region_9.10 | all-reduce | flops 96 | bytes 768 | tf_op jit(solution)/shard_map/psum | solution.py:119
  99.1 0.6 convolution_convert_fusion.1
  99.7 0.6 copy.113
  100.3 34.2 %all_to_all.10 = bf16[8,1,96,720]{3,2,1,0:T(8,128)(2,1)S(1)} all-to-all(bf16[8,1,96,720]{3,2,1,0:T(8,128)(2,1)S(1)} %bitcast.103), channel_id=1, replica_groups=mesh['dp'=8,'tp'=4] {'dp'}, dimensions={0} | all-to-all | bytes 2211840 | tf_op jit(solution)/shard_map/all_to_all | solution.py:143
  134.6 1.9 copy.115
  136.5 42.0 %all-gather.3.cloned.1.call-done = bf16[8,1,96,2880]{2,0,1,3:T(8,128)(2,1)} async-done(((bf16[8,1,96,720]{2,0,1,3:T(8,128)(2,1)}), bf16[8,1,96,2880]{2,0,1,3:T(8,128)(2,1)}) %all-gather.3.cloned.1.call-update) | async-done | bytes 4423696 | tf_op jit(solution)/shard_map/all_gather | solution.py:142
  178.5 8.3 %copy.116 = bf16[8,1,96,2880]{3,2,0,1:T(8,128)(2,1)} copy(bf16[8,1,96,2880]{2,0,1,3:T(8,128)(2,1)} %all-gather.3.cloned.1.call-done) | data formatting | bytes 8847360 | tf_op jit(solution)/shard_map/all_gather | solution.py:142
  186.8 11.4 %fusion.2 = f32[8,1,96,1440]{3,2,0,1:T(8,128)S(1)} fusion(bf16[2880,1440,1]{0,1,2:T(8,128)(2,1)} %bitcast.119, bf16[8,1,96,2880]{3,2,0,1:T(8,128)(2,1)} %copy.116), kind=kOutput, calls=%fused_computation.3 | convolution fusion | flops 6370099200 | bytes 17141760 | tf_op jit(solution)/shard_map/gecd,edf->gecf/dot_general | solution.py:140
  198.2 0.8 fusion.10
  199.1 0.3 collective-permute-start
  199.4 15.4 %collective-permute-done = bf16[8,1,96,720]{3,2,0,1:T(8,128)(2,1)S(1)} collective-permute-done((bf16[8,1,96,720]{3,2,0,1:T(8,128)(2,1)S(1)}, bf16[8,1,96,720]{3,2,0,1:T(8,128)(2,1)S(1)}, u32[]{:S(2)}, u32[]{:S(2)}) %collective-permute-start) | collective-permute-done | bytes 1105952 | tf_op jit(solution)/shard_map/ppermute | solution.py:16
  214.8 15.7 %collective-permute-done.1 = bf16[8,1,96,720]{3,2,0,1:T(8,128)(2,1)} collective-permute-done((bf16[8,1,96,720]{3,2,0,1:T(8,128)(2,1)S(1)}, bf16[8,1,96,720]{3,2,0,1:T(8,128)(2,1)}, u32[]{:S(2)}, u32[]{:S(2)}) %collective-permute-start.1) | collective-permute-done | bytes 1105952 | tf_op jit(solution)/shard_map/ppermute | solution.py:16
  230.5 2.5 fusion.25
  233.0 2.5 fusion.23
  235.5 2.9 fusion.21
  238.4 8.0 %collective-permute-done.2 = bf16[8,1,96,720]{3,2,0,1:T(8,128)(2,1)} collective-permute-done((bf16[8,1,96,720]{3,2,0,1:T(8,128)(2,1)}, bf16[8,1,96,720]{3,2,0,1:T(8,128)(2,1)}, u32[]{:S(2)}, u32[]{:S(2)}) %collective-permute-start.2) | collective-permute-done | bytes 1105952 | tf_op jit(solution)/shard_map/ppermute | solution.py:16
  246.4 4.1 %fusion.13 = bf16[8,1,96,720]{3,2,1,0:T(8,128)(2,1)} fusion(f32[720,8,96]{0,2,1:T(8,128)S(1)} %fusion.21, f32[720,8,96]{0,2,1:T(8,128)S(1)} %fusion.25, f32[720,8,96]{0,2,1:T(8,128)S(1)} %fusion.23, bf16[8,1,96,720]{3,2,0,1:T(8,128)(2,1)} %collective-permute-done.2, bf16[1,2880,720]{1,2,0:T(8,128)(2,1)} %param.24, s32[]{:T(128)S(6)} %select_n.81), kind=kOutput, calls=%fused_computation.16 | convolution fusion | flops 798474240 | bytes 10027012 | tf_op jit(solution)/shard_map/gecf,efd->gecd/dot_general | solution.py:166
  250.6 5.7 %all-to-all-start.1 = ((bf16[8,1,96,720]{3,2,1,0:T(8,128)(2,1)}), bf16[8,1,96,720]{3,2,1,0:T(8,128)(2,1)}, u32[]{:S(2)}, u32[]{:S(2)}) async-start(bf16[8,1,96,720]{3,2,1,0:T(8,128)(2,1)} %fusion.13), calls=%async_computation.1 | async-start | bytes 2359296 | tf_op jit(solution)/shard_map/all_to_all | solution.py:173
  256.2 0.3 fusion.44
  256.5 6.1 %psum.23 = f32[96,8]{0,1:T(8,128)S(1)} all-reduce(f32[96,8]{0,1:T(8,128)S(1)} %fusion.44), channel_id=1, replica_groups=mesh['dp'=8,'tp'=4] {'tp'}, use_global_device_ids=true, to_apply=%region_10.11 | all-reduce | flops 768 | bytes 6144 | tf_op jit(solution)/shard_map/psum | solution.py:122
  262.7 0.2 select_reduce_fusion
  262.9 20.6 %all-to-all-done.1 = bf16[8,1,96,720]{3,2,1,0:T(8,128)(2,1)} async-done(((bf16[8,1,96,720]{3,2,1,0:T(8,128)(2,1)}), bf16[8,1,96,720]{3,2,1,0:T(8,128)(2,1)}, u32[]{:S(2)}, u32[]{:S(2)}) %all-to-all-start.1) | async-done | bytes 1105952 | tf_op jit(solution)/shard_map/all_to_all | solution.py:173
  283.5 2.7 convolution_add_fusion
  (44 shorter events, 0.7 us)
Async XLA Ops:
  6.5 57.3 %copy-start = (bf16[512,2880]{0,1:T(8,128)(2,1)S(1)}, bf16[512,2880]{0,1:T(8,128)(2,1)}, u32[]{:S(2)}) copy-start(bf16[512,2880]{0,1:T(8,128)(2,1)} %param.18) | copy-start | bytes 8847364
  6.5 21.1 %copy-start.7 = (s32[96]{0:T(128)S(1)}, s32[96]{0:T(128)}, u32[]{:S(2)}) copy-start(s32[96]{0:T(128)} %param.20) | copy-start | bytes 1156
  6.5 85.6 %reduce-scatter.4.cloned.1.call-start = ((), (), s32[]{:S(2)}) async-start(), calls=%async_computation.4 | async-start | bytes 921600
  27.6 7.7 %copy-start.4 = (bf16[2880,96,1]{0,1,2:T(8,128)(2,1)S(1)}, bf16[2880,96,1]{0,1,2:T(8,128)(2,1)}, u32[]{:S(2)}) copy-start(bf16[2880,96,1]{0,1,2:T(8,128)(2,1)} %reshape.278) | copy-start | bytes 1658884
  40.4 8.7 %copy-start.3 = (bf16[2880,96]{0,1:T(8,128)(2,1)S(1)}, bf16[2880,96]{0,1:T(8,128)(2,1)}, u32[]{:S(2)}) copy-start(bf16[2880,96]{0,1:T(8,128)(2,1)} %reshape.277) | copy-start | bytes 1658884
  49.1 3.5 %copy-start.9 = (f32[8]{0:T(128)S(1)}, f32[8]{0:T(128)}, u32[]{:S(2)}) copy-start(f32[8]{0:T(128)} %param.17) | copy-start | bytes 100
  52.7 7.2 %copy-start.6 = (pred[96,128]{1,0:T(8,128)(4,1)S(1)}, pred[96,128]{1,0:T(8,128)(4,1)}, u32[]{:S(2)}) copy-start(pred[96,128]{1,0:T(8,128)(4,1)} %fusion.57) | copy-start | bytes 36868
  63.8 4.2 %copy-start.5 = (s32[96,4]{0,1:T(4,128)S(1)}, s32[96,4]{0,1:T(4,128)}, u32[]{:S(2)}) copy-start(s32[96,4]{0,1:T(4,128)} %param.25) | copy-start | bytes 4612
  63.8 29.4 %copy-start.2 = (bf16[96,720]{1,0:T(8,128)(2,1)S(1)}, bf16[96,720]{1,0:T(8,128)(2,1)}, u32[]{:S(2)}) copy-start(bf16[96,720]{1,0:T(8,128)(2,1)} %param.13) | copy-start | bytes 414724
  67.9 110.5 %all-gather.3.cloned.1.call-start = ((), (), s32[]{:S(2)}) async-start(), calls=%async_computation.3 | async-start | bytes 7372800 | tf_op jit(solution)/shard_map/all_gather | solution.py:142
  199.1 15.7 %collective-permute-start = (bf16[8,1,96,720]{3,2,0,1:T(8,128)(2,1)S(1)}, bf16[8,1,96,720]{3,2,0,1:T(8,128)(2,1)S(1)}, u32[]{:S(2)}, u32[]{:S(2)}) collective-permute-start(bf16[8,1,96,720]{3,2,0,1:T(8,128)(2,1)S(1)} %fusion.10), channel_id=1, source_target_pairs={{0,1},{1,2},{2,3},{3,0},{4,5},{5,6},{6,7},{7,4},{8,9},{9,10},{10,1... | collective-permute-start | bytes 3317768 | tf_op jit(solution)/shard_map/ppermute | solution.py:16
  214.8 15.7 %collective-permute-start.1 = (bf16[8,1,96,720]{3,2,0,1:T(8,128)(2,1)S(1)}, bf16[8,1,96,720]{3,2,0,1:T(8,128)(2,1)}, u32[]{:S(2)}, u32[]{:S(2)}) collective-permute-start(bf16[8,1,96,720]{3,2,0,1:T(8,128)(2,1)S(1)} %collective-permute-done), channel_id=1, source_target_pairs={{0,1},{1,2},{2,3},{3,0},{4,5},{5,6},{6,7},{7,4},{8,9},{9,10},{10,1... | collective-permute-start | bytes 3317768 | tf_op jit(solution)/shard_map/ppermute | solution.py:16
  230.5 15.9 %collective-permute-start.2 = (bf16[8,1,96,720]{3,2,0,1:T(8,128)(2,1)}, bf16[8,1,96,720]{3,2,0,1:T(8,128)(2,1)}, u32[]{:S(2)}, u32[]{:S(2)}) collective-permute-start(bf16[8,1,96,720]{3,2,0,1:T(8,128)(2,1)} %collective-permute-done.1), channel_id=1, source_target_pairs={{0,1},{1,2},{2,3},{3,0},{4,5},{5,6},{6,7},{7,4},{8,9},{9,10},{10,1... | collective-permute-start | bytes 3317768 | tf_op jit(solution)/shard_map/ppermute | solution.py:16
  246.4 39.7 %copy-start.1 = (bf16[512,2880]{0,1:T(8,128)(2,1)S(1)}, bf16[512,2880]{0,1:T(8,128)(2,1)}, u32[]{:S(2)}) copy-start(bf16[512,2880]{0,1:T(8,128)(2,1)} %param.18) | copy-start | bytes 8847364
  250.6 5.7 %copy-start.8 = (bf16[720,8]{0,1:T(8,128)(2,1)S(1)}, bf16[720,8]{0,1:T(8,128)(2,1)}, u32[]{:S(2)}) copy-start(bf16[720,8]{0,1:T(8,128)(2,1)} %param.22) | copy-start | bytes 34564
  250.6 32.9 %all-to-all-start.1 = ((bf16[8,1,96,720]{3,2,1,0:T(8,128)(2,1)}), bf16[8,1,96,720]{3,2,1,0:T(8,128)(2,1)}, u32[]{:S(2)}, u32[]{:S(2)}) async-start(bf16[8,1,96,720]{3,2,1,0:T(8,128)(2,1)} %fusion.13), calls=%async_computation.1 | async-start | bytes 2359296 | tf_op jit(solution)/shard_map/all_to_all | solution.py:173
Sparse Core Ops, SparseCore 0:
  68.0 24.0 reduce-scatter.3
  136.6 41.8 all-gather.2
